TPU v7x, 32 devices: a whole 2x2x4 slice. The times are simulated.
32 devices in a mesh: ctx: 8 (over z, x), heads: 4 (over y, core).
Axes of the slice: x: 2, y: 2, z: 4, core: 2. Of those that a mesh axis runs over, the one named last changes fastest.
Arguments:
- query_rows: bfloat16 [8, 16, 2, 128], P('ctx', 'heads'), may hold values from -6 to 6
- past_keys: bfloat16 [8, 16, 512, 128], P(None, 'heads', 'ctx'), may hold values from -6 to 6
- past_values: bfloat16 [8, 16, 512, 128], P(None, 'heads', 'ctx'), may hold values from -6 to 6
- used_length: int32 [8], replicated, may hold values from 256 to 512
Outputs:
- read: bfloat16 [8, 16, 2, 128], P('ctx', 'heads')
All inputs are finite; a program needn't handle non-finite values.
Results may differ from a plain program's by a relative error of at most 0.0015.
Values may be sent and summed in bfloat16 or wider, within the bound.
A program may use at most 64 MiB of HBM per device.

v0:
```python
import jax
import jax.numpy as jnp
from jax import lax
from jax.sharding import PartitionSpec as P

HEAD_SIZE = 128


def local(query_rows, past_keys, past_values, used_length):
    all_queries = lax.all_gather(query_rows, "ctx", axis=0, tiled=True)
    logit = jnp.einsum(
        "bkgd,bktd->bkgt", all_queries, past_keys, preferred_element_type=jnp.float32
    ) * HEAD_SIZE ** (-0.5)
    positions = lax.axis_index("ctx") * past_keys.shape[2] + jnp.arange(past_keys.shape[2])
    filled = positions[None, :] < used_length[:, None]
    logit = jnp.where(filled[:, None, None, :], logit, -1e30)
    top = jnp.max(logit, axis=-1)
    part = jnp.where(filled[:, None, None, :], jnp.exp(logit - top[..., None]), 0.0)
    weight_sum = jnp.sum(part, axis=-1)
    read_sum = jnp.einsum(
        "bkgt,bktd->bkgd", part, past_values.astype(jnp.float32), precision=lax.Precision.HIGHEST
    )
    tops, sums, parts = (
        lax.all_to_all(top[None], "ctx", split_axis=1, concat_axis=0, tiled=True),
        lax.all_to_all(weight_sum[None], "ctx", split_axis=1, concat_axis=0, tiled=True),
        lax.all_to_all(read_sum[None], "ctx", split_axis=1, concat_axis=0, tiled=True),
    )
    best = jnp.max(tops, axis=0)
    scale = jnp.exp(tops - best)
    weight_own = jnp.sum(sums * scale, axis=0)
    read_own = jnp.sum(parts * scale[..., None], axis=0)
    read = (read_own / weight_own[..., None]).astype(jnp.bfloat16)
    return read


def solution(mesh):
    return jax.shard_map(
        local,
        mesh=mesh,
        in_specs=(
            P("ctx", "heads", None, None),
            P(None, "heads", "ctx", None),
            P(None, "heads", "ctx", None),
            P(),
        ),
        out_specs=P("ctx", "heads", None, None),
        check_vma=False,
    )
```

profile of v0, /device:TPU:0, one launch (start us, length us, event | category | flops | bytes accessed | tf_op | source)
XLA Modules:
  0.0 62.1 jit_solution(10074065572557208397)
XLA Ops:
  0.0 0.0 copy-start
  0.0 0.7 %copy-done.1 = bf16[1,4,2,128]{3,2,1,0:T(2,128)(2,1)S(1)} copy-done((bf16[1,4,2,128]{3,2,1,0:T(2,128)(2,1)S(1)}, bf16[1,4,2,128]{3,2,1,0:T(2,128)(2,1)}, u32[]{:S(2)}) %copy-start.1) | copy-done | bytes 2072
  0.8 28.1 %all_gather.3 = bf16[8,4,2,128]{3,1,2,0:T(4,128)(2,1)S(1)} all-gather(bf16[1,4,2,128]{3,1,2,0:T(4,128)(2,1)S(1)} %copy.7), channel_id=1, replica_groups=mesh['ctx'=8,'heads'=4] {'ctx'}, dimensions={0}, use_global_device_ids=true | all-gather | bytes 18432 | tf_op jit(solution)/shard_map/all_gather | solution.py:10
  28.8 0.0 copy-done.2
  28.8 0.1 broadcast_compare_fusion
  28.9 1.5 %fusion.10 = (f32[8,4,2]{2,1,0:T(4,128)S(1)}, f32[8,4,2,64]{3,2,1,0:T(2,128)S(1)}) fusion(bf16[8,4,64,128]{3,2,1,0:T(8,128)(2,1)} %param.5, bf16[8,4,2,128]{3,1,2,0:T(4,128)(2,1)S(1)} %all_gather.3, pred[8,64]{1,0:T(8,128)(4,1)S(1)} %broadcast_compare_fusion), kind=kOutput, calls=%fused_computation.19 | convolution fusion | flops 1060800 | bytes 557824 | tf_op jit(solution)/shard_map/bkgd,bktd->bkgt/dot_general | solution.py:11
  30.4 0.7 %copy.11 = f32[1,8,4,2]{2,3,0,1:T(2,128)} copy(f32[1,8,4,2]{3,2,1,0:T(4,128)S(1)} %bitcast.30) | data formatting | bytes 512 | tf_op jit(solution)/shard_map/broadcast_in_dim | solution.py:24
  31.1 4.0 %all-to-all-start.1 = ((f32[1,8,4,2]{2,3,0,1:T(2,128)}), f32[1,8,4,2]{2,3,0,1:T(2,128)S(1)}, u32[]{:S(2)}, u32[]{:S(2)}) async-start(f32[1,8,4,2]{2,3,0,1:T(2,128)} %copy.11), calls=%async_computation.1 | async-start | bytes 16384 | tf_op jit(solution)/shard_map/all_to_all | solution.py:24
  35.1 1.2 %convolution_bitcast_fusion = f32[1,8,4,2,128]{4,3,2,0,1:T(2,128)} fusion(bf16[8,4,64,128]{3,2,1,0:T(8,128)(2,1)S(1)} %copy-done, f32[8,4,2,64]{3,2,1,0:T(2,128)S(1)} %get-tuple-element.6, pred[8,64]{1,0:T(8,128)(4,1)S(1)} %broadcast_compare_fusion, f32[8,4,2]{2,1,0:T(4,128)S(1)} %get-tuple-element.5), kind=kOutput, calls=%fused_computation | convolution fusion | flops 6299648 | bytes 574208 | tf_op jit(solution)/shard_map/bkgt,bktd->bkgd/dot_general | solution.py:20
  36.3 0.2 fusion.8
  36.5 0.7 %copy.15 = f32[1,8,4,2]{2,3,0,1:T(2,128)} copy(f32[1,8,4,2]{3,2,1,0:T(4,128)S(1)} %bitcast.31) | data formatting | bytes 512 | tf_op jit(solution)/shard_map/broadcast_in_dim | solution.py:25
  37.2 4.4 %all-to-all-done.1 = f32[1,8,4,2]{2,3,0,1:T(2,128)S(1)} async-done(((f32[1,8,4,2]{2,3,0,1:T(2,128)}), f32[1,8,4,2]{2,3,0,1:T(2,128)S(1)}, u32[]{:S(2)}, u32[]{:S(2)}) %all-to-all-start.1) | async-done | bytes 288 | tf_op jit(solution)/shard_map/all_to_all | solution.py:24
  41.6 3.3 %all-to-all-start.2 = ((f32[1,8,4,2]{2,3,0,1:T(2,128)}), f32[1,8,4,2]{2,3,0,1:T(2,128)S(1)}, u32[]{:S(2)}, u32[]{:S(2)}) async-start(f32[1,8,4,2]{2,3,0,1:T(2,128)} %copy.15), calls=%async_computation.2 | async-start | bytes 16384 | tf_op jit(solution)/shard_map/all_to_all | solution.py:25
  44.9 0.1 copy.12
  45.0 0.1 fusion.6
  45.1 6.3 %all-to-all-done.2 = f32[1,8,4,2]{2,3,0,1:T(2,128)S(1)} async-done(((f32[1,8,4,2]{2,3,0,1:T(2,128)}), f32[1,8,4,2]{2,3,0,1:T(2,128)S(1)}, u32[]{:S(2)}, u32[]{:S(2)}) %all-to-all-start.2) | async-done | bytes 288 | tf_op jit(solution)/shard_map/all_to_all | solution.py:25
  51.4 3.3 %all-to-all-start = ((f32[1,8,4,2,128]{4,3,2,0,1:T(2,128)}), f32[1,8,4,2,128]{4,3,2,0,1:T(2,128)S(1)}, u32[]{:S(2)}, u32[]{:S(2)}) async-start(f32[1,8,4,2,128]{4,3,2,0,1:T(2,128)} %convolution_bitcast_fusion), calls=%async_computation | async-start | bytes 65536 | tf_op jit(solution)/shard_map/all_to_all | solution.py:26
  54.7 0.1 copy.16
  54.8 0.2 fusion.5
  55.0 0.1 copy.18
  55.1 0.1 copy.13
  55.2 6.2 %all-to-all-done = f32[1,8,4,2,128]{4,3,2,0,1:T(2,128)S(1)} async-done(((f32[1,8,4,2,128]{4,3,2,0,1:T(2,128)}), f32[1,8,4,2,128]{4,3,2,0,1:T(2,128)S(1)}, u32[]{:S(2)}, u32[]{:S(2)}) %all-to-all-start) | async-done | bytes 32800 | tf_op jit(solution)/shard_map/all_to_all | solution.py:26
  61.4 0.1 fusion.1
  61.5 0.7 %fusion.7 = bf16[1,4,2,128]{3,2,1,0:T(2,128)(2,1)} fusion(f32[4,2,128]{2,1,0:T(2,128)S(1)} %fusion.1, f32[4,2]{1,0:T(4,128)S(1)} %copy.18), kind=kLoop, calls=%fused_computation.14 | loop fusion | flops 2048 | bytes 6176 | tf_op jit(solution)/shard_map/convert_element_type | solution.py:32
  (6 shorter events, 0.0 us)
Async XLA Ops:
  0.0 35.1 %copy-start = (bf16[8,4,64,128]{3,2,1,0:T(8,128)(2,1)S(1)}, bf16[8,4,64,128]{3,2,1,0:T(8,128)(2,1)}, u32[]{:S(2)}) copy-start(bf16[8,4,64,128]{3,2,1,0:T(8,128)(2,1)} %param.6) | copy-start | bytes 1572868
  0.0 0.7 %copy-start.1 = (bf16[1,4,2,128]{3,2,1,0:T(2,128)(2,1)S(1)}, bf16[1,4,2,128]{3,2,1,0:T(2,128)(2,1)}, u32[]{:S(2)}) copy-start(bf16[1,4,2,128]{3,2,1,0:T(2,128)(2,1)} %param.4) | copy-start | bytes 6148
  0.7 28.1 %copy-start.2 = (s32[8]{0:T(128)S(1)}, s32[8]{0:T(128)}, u32[]{:S(2)}) copy-start(s32[8]{0:T(128)} %param.7) | copy-start | bytes 100
  31.1 10.5 %all-to-all-start.1 = ((f32[1,8,4,2]{2,3,0,1:T(2,128)}), f32[1,8,4,2]{2,3,0,1:T(2,128)S(1)}, u32[]{:S(2)}, u32[]{:S(2)}) async-start(f32[1,8,4,2]{2,3,0,1:T(2,128)} %copy.11), calls=%async_computation.1 | async-start | bytes 16384 | tf_op jit(solution)/shard_map/all_to_all | solution.py:24
  41.6 9.8 %all-to-all-start.2 = ((f32[1,8,4,2]{2,3,0,1:T(2,128)}), f32[1,8,4,2]{2,3,0,1:T(2,128)S(1)}, u32[]{:S(2)}, u32[]{:S(2)}) async-start(f32[1,8,4,2]{2,3,0,1:T(2,128)} %copy.15), calls=%async_computation.2 | async-start | bytes 16384 | tf_op jit(solution)/shard_map/all_to_all | solution.py:25
  51.4 10.0 %all-to-all-start = ((f32[1,8,4,2,128]{4,3,2,0,1:T(2,128)}), f32[1,8,4,2,128]{4,3,2,0,1:T(2,128)S(1)}, u32[]{:S(2)}, u32[]{:S(2)}) async-start(f32[1,8,4,2,128]{4,3,2,0,1:T(2,128)} %convolution_bitcast_fusion), calls=%async_computation | async-start | bytes 65536 | tf_op jit(solution)/shard_map/all_to_all | solution.py:26
where the time goes:
time: 62.5 us; the launch traced here: 62.1 us
  blocking collectives  28.1 us (45%)
  waiting for transfers between devices  16.8 us (27%)
  starting transfers between devices  10.6 us (17%)
  matrix products  2.71 us (4%)
  local copies, waits for them, and re-layouts  2.59 us (4%)
  other arithmetic  1.32 us (2%)
    all_gather x1, blocking collectives, local(): all_queries = lax.all_gather(query_rows, 'ctx', axis=0, tiled=True)  28.1 us
    all_to_all x1, waiting for transfers between devices, local(): lax.all_to_all(weight_sum[None], 'ctx', split_axis=1, concat_axis=0, tile...  6.27 us
    all_to_all x1, waiting for transfers between devices, local(): lax.all_to_all(read_sum[None], 'ctx', split_axis=1, concat_axis=0, tiled=...  6.17 us
    all_to_all x1, waiting for transfers between devices, local(): lax.all_to_all(top[None], 'ctx', split_axis=1, concat_axis=0, tiled=True)  4.37 us
    all_to_all x1, starting transfers between devices, local(): lax.all_to_all(top[None], 'ctx', split_axis=1, concat_axis=0, tiled=True)  3.97 us
    all_to_all x1, starting transfers between devices, local(): lax.all_to_all(read_sum[None], 'ctx', split_axis=1, concat_axis=0, tiled=...  3.33 us
    all_to_all x1, starting transfers between devices, local(): lax.all_to_all(weight_sum[None], 'ctx', split_axis=1, concat_axis=0, tile...  3.32 us
    dot_general x1, matrix products, local(): jnp.einsum('bkgd,bktd->bkgt', all_queries, past_keys, preferred_element_t...  1.51 us
  transfers between devices with their start and end apart: 3, of which 3 were waited for; matrix products, arithmetic and copies ran while one was open for 4% of the time, Pallas kernels for 0%

commit v1 on v0

--- a/solution.py
+++ b/solution.py
@@ -21,7 +21,12 @@
         "bkgt,bktd->bkgd", part, past_values.astype(jnp.float32), precision=lax.Precision.HIGHEST
     )
     tops, sums, parts = (
-        lax.all_to_all(top[None], "ctx", split_axis=1, concat_axis=0, tiled=True),
+        jnp.concatenate(
+            lax.all_to_all(
+                jnp.stack(jnp.split(top[None], lax.axis_size("ctx"), axis=1)), "ctx", 0, 0
+            ),
+            axis=0,
+        ),
         lax.all_to_all(weight_sum[None], "ctx", split_axis=1, concat_axis=0, tiled=True),
         lax.all_to_all(read_sum[None], "ctx", split_axis=1, concat_axis=0, tiled=True),
     )

time: 62.5 us -> 66.6 us (1.066)
  local copies, waits for them, and re-layouts: 2.59 us -> 6.7 us
    unnamed x7 -> x14, local copies, waits for them, and re-layouts: 0.75 us -> 4.72 us
    broadcast_in_dim x1 -> x0, local copies, waits for them, and re-layouts: 0.73 us -> none  [local(): top[None]]
where the time goes in v1:
time: 66.6 us; the launch traced here: 66.2 us
  blocking collectives  28.1 us (42%)
  waiting for transfers between devices  16.8 us (25%)
  starting transfers between devices  10.6 us (16%)
  local copies, waits for them, and re-layouts  6.7 us (10%)
  matrix products  2.71 us (4%)
  other arithmetic  1.32 us (2%)
    all_gather x1, blocking collectives, local(): all_queries = lax.all_gather(query_rows, 'ctx', axis=0, tiled=True)  28.1 us
    all_to_all x1, waiting for transfers between devices, local(): lax.all_to_all(weight_sum[None], 'ctx', split_axis=1, concat_axis=0, tile...  6.27 us
    all_to_all x1, waiting for transfers between devices, local(): lax.all_to_all(read_sum[None], 'ctx', split_axis=1, concat_axis=0, tiled=...  6.17 us
    unnamed x14, local copies, waits for them, and re-layouts  4.72 us
    all_to_all x1, waiting for transfers between devices, local(): lax.all_to_all(jnp.stack(jnp.split(top[None], lax.axis_size('ctx'), axis=...  4.36 us
    all_to_all x1, starting transfers between devices, local(): lax.all_to_all(jnp.stack(jnp.split(top[None], lax.axis_size('ctx'), axis=...  3.97 us
    all_to_all x1, starting transfers between devices, local(): lax.all_to_all(read_sum[None], 'ctx', split_axis=1, concat_axis=0, tiled=...  3.33 us
    all_to_all x1, starting transfers between devices, local(): lax.all_to_all(weight_sum[None], 'ctx', split_axis=1, concat_axis=0, tile...  3.32 us
  transfers between devices with their start and end apart: 3, of which 3 were waited for; matrix products, arithmetic and copies ran while one was open for 4% of the time, Pallas kernels for 0%

profile of v1, /device:TPU:0, one launch (start us, length us, event | category | flops | bytes accessed | tf_op | source)
XLA Modules:
  0.0 66.2 jit_solution(1190781156331781300)
XLA Ops:
  0.0 0.7 %copy-done.1 = bf16[1,4,2,128]{3,2,1,0:T(2,128)(2,1)S(1)} copy-done((bf16[1,4,2,128]{3,2,1,0:T(2,128)(2,1)S(1)}, bf16[1,4,2,128]{3,2,1,0:T(2,128)(2,1)}, u32[]{:S(2)}) %copy-start.1) | copy-done | bytes 2072
  0.8 28.1 %all_gather.3 = bf16[8,4,2,128]{3,1,2,0:T(4,128)(2,1)S(1)} all-gather(bf16[1,4,2,128]{3,1,2,0:T(4,128)(2,1)S(1)} %copy.13), channel_id=1, replica_groups=mesh['ctx'=8,'heads'=4] {'ctx'}, dimensions={0}, use_global_device_ids=true | all-gather | bytes 18432 | tf_op jit(solution)/shard_map/all_gather | solution.py:10
  28.9 1.5 %fusion.10 = (f32[8,4,2]{2,1,0:T(4,128)S(1)}, f32[8,4,2,64]{3,2,1,0:T(2,128)S(1)}) fusion(bf16[8,4,64,128]{3,2,1,0:T(8,128)(2,1)} %param.5, bf16[8,4,2,128]{3,1,2,0:T(4,128)(2,1)S(1)} %all_gather.3, pred[8,64]{1,0:T(8,128)(4,1)S(1)} %broadcast_compare_fusion), kind=kOutput, calls=%fused_computation.35 | convolution fusion | flops 1060800 | bytes 557824 | tf_op jit(solution)/shard_map/bkgd,bktd->bkgt/dot_general | solution.py:11
  30.4 0.1 copy.16
  30.5 0.2 slice_reduce_fusion
  30.7 0.6 constant_dynamic-update-slice_fusion.7
  31.3 0.5 constant_dynamic-update-slice_fusion.6
  31.8 0.6 constant_dynamic-update-slice_fusion.5
  32.4 0.6 constant_dynamic-update-slice_fusion.4
  33.0 0.5 constant_dynamic-update-slice_fusion.3
  33.5 0.6 constant_dynamic-update-slice_fusion.2
  34.1 0.6 constant_dynamic-update-slice_fusion.1
  34.7 0.6 constant_dynamic-update-slice_fusion
  35.2 4.0 %all-to-all-start.1 = ((f32[8,1,1,4,2]{3,4,2,1,0:T(2,128)}), f32[8,1,1,4,2]{3,4,2,1,0:T(2,128)S(1)}, u32[]{:S(2)}, u32[]{:S(2)}) async-start(f32[8,1,1,4,2]{3,4,2,1,0:T(2,128)} %constant_dynamic-update-slice_fusion), calls=%async_computation.1 | async-start | bytes 16384 | tf_op jit(solution)/shard_map/all_to_all | solution.py:25
  39.2 1.2 %convolution_bitcast_fusion = f32[1,8,4,2,128]{4,3,2,0,1:T(2,128)} fusion(bf16[8,4,64,128]{3,2,1,0:T(8,128)(2,1)S(1)} %copy-done, f32[8,4,2,64]{3,2,1,0:T(2,128)S(1)} %get-tuple-element.14, pred[8,64]{1,0:T(8,128)(4,1)S(1)} %broadcast_compare_fusion, f32[8,4,2]{2,1,0:T(4,128)S(1)} %get-tuple-element.13), kind=kOutput, calls=%fused_computation | convolution fusion | flops 6299648 | bytes 574208 | tf_op jit(solution)/shard_map/bkgt,bktd->bkgd/dot_general | solution.py:20
  40.4 0.2 fusion.8
  40.6 0.7 %copy.20 = f32[1,8,4,2]{2,3,0,1:T(2,128)} copy(f32[1,8,4,2]{3,2,1,0:T(4,128)S(1)} %bitcast.47) | data formatting | bytes 512 | tf_op jit(solution)/shard_map/broadcast_in_dim | solution.py:30
  41.4 4.4 %all-to-all-done.1 = f32[8,1,1,4,2]{3,4,2,1,0:T(2,128)S(1)} async-done(((f32[8,1,1,4,2]{3,4,2,1,0:T(2,128)}), f32[8,1,1,4,2]{3,4,2,1,0:T(2,128)S(1)}, u32[]{:S(2)}, u32[]{:S(2)}) %all-to-all-start.1) | async-done | bytes 288 | tf_op jit(solution)/shard_map/all_to_all | solution.py:25
  45.7 3.3 %all-to-all-start.2 = ((f32[1,8,4,2]{2,3,0,1:T(2,128)}), f32[1,8,4,2]{2,3,0,1:T(2,128)S(1)}, u32[]{:S(2)}, u32[]{:S(2)}) async-start(f32[1,8,4,2]{2,3,0,1:T(2,128)} %copy.20), calls=%async_computation.2 | async-start | bytes 16384 | tf_op jit(solution)/shard_map/all_to_all | solution.py:30
  49.2 6.3 %all-to-all-done.2 = f32[1,8,4,2]{2,3,0,1:T(2,128)S(1)} async-done(((f32[1,8,4,2]{2,3,0,1:T(2,128)}), f32[1,8,4,2]{2,3,0,1:T(2,128)S(1)}, u32[]{:S(2)}, u32[]{:S(2)}) %all-to-all-start.2) | async-done | bytes 288 | tf_op jit(solution)/shard_map/all_to_all | solution.py:30
  55.5 3.3 %all-to-all-start = ((f32[1,8,4,2,128]{4,3,2,0,1:T(2,128)}), f32[1,8,4,2,128]{4,3,2,0,1:T(2,128)S(1)}, u32[]{:S(2)}, u32[]{:S(2)}) async-start(f32[1,8,4,2,128]{4,3,2,0,1:T(2,128)} %convolution_bitcast_fusion), calls=%async_computation | async-start | bytes 65536 | tf_op jit(solution)/shard_map/all_to_all | solution.py:31
  58.9 0.2 fusion.5
  59.3 6.2 %all-to-all-done = f32[1,8,4,2,128]{4,3,2,0,1:T(2,128)S(1)} async-done(((f32[1,8,4,2,128]{4,3,2,0,1:T(2,128)}), f32[1,8,4,2,128]{4,3,2,0,1:T(2,128)S(1)}, u32[]{:S(2)}, u32[]{:S(2)}) %all-to-all-start) | async-done | bytes 32800 | tf_op jit(solution)/shard_map/all_to_all | solution.py:31
  65.6 0.7 fusion.7
  (15 shorter events, 0.7 us)
Async XLA Ops:
  0.0 39.2 %copy-start = (bf16[8,4,64,128]{3,2,1,0:T(8,128)(2,1)S(1)}, bf16[8,4,64,128]{3,2,1,0:T(8,128)(2,1)}, u32[]{:S(2)}) copy-start(bf16[8,4,64,128]{3,2,1,0:T(8,128)(2,1)} %param.6) | copy-start | bytes 1572868
  0.0 0.7 %copy-start.1 = (bf16[1,4,2,128]{3,2,1,0:T(2,128)(2,1)S(1)}, bf16[1,4,2,128]{3,2,1,0:T(2,128)(2,1)}, u32[]{:S(2)}) copy-start(bf16[1,4,2,128]{3,2,1,0:T(2,128)(2,1)} %param.4) | copy-start | bytes 6148
  0.7 28.1 %copy-start.2 = (s32[8]{0:T(128)S(1)}, s32[8]{0:T(128)}, u32[]{:S(2)}) copy-start(s32[8]{0:T(128)} %param.7) | copy-start | bytes 100
  35.2 10.5 %all-to-all-start.1 = ((f32[8,1,1,4,2]{3,4,2,1,0:T(2,128)}), f32[8,1,1,4,2]{3,4,2,1,0:T(2,128)S(1)}, u32[]{:S(2)}, u32[]{:S(2)}) async-start(f32[8,1,1,4,2]{3,4,2,1,0:T(2,128)} %constant_dynamic-update-slice_fusion), calls=%async_computation.1 | async-start | bytes 16384 | tf_op jit(solution)/shard_map/all_to_all | solution.py:25
  45.7 9.8 %all-to-all-start.2 = ((f32[1,8,4,2]{2,3,0,1:T(2,128)}), f32[1,8,4,2]{2,3,0,1:T(2,128)S(1)}, u32[]{:S(2)}, u32[]{:S(2)}) async-start(f32[1,8,4,2]{2,3,0,1:T(2,128)} %copy.20), calls=%async_computation.2 | async-start | bytes 16384 | tf_op jit(solution)/shard_map/all_to_all | solution.py:30
  55.5 10.0 %all-to-all-start = ((f32[1,8,4,2,128]{4,3,2,0,1:T(2,128)}), f32[1,8,4,2,128]{4,3,2,0,1:T(2,128)S(1)}, u32[]{:S(2)}, u32[]{:S(2)}) async-start(f32[1,8,4,2,128]{4,3,2,0,1:T(2,128)} %convolution_bitcast_fusion), calls=%async_computation | async-start | bytes 65536 | tf_op jit(solution)/shard_map/all_to_all | solution.py:31
